TPU v7x, 32 devices: a whole 2x2x4 slice. The times are simulated.
32 devices in a mesh: fsdp: 8 (over z, core), tp: 4 (over y, x).
Axes of the slice: x: 2, y: 2, z: 4, core: 2. Of those that a mesh axis runs over, the one named last changes fastest.
Arguments:
- tokens: bfloat16 [80, 16384], P('tp', 'fsdp'), may hold values from -6 to 6
- gate_weight: bfloat16 [16384, 28672], P('fsdp', 'tp'), may hold values from -0.046875 to 0.046875
- up_weight: bfloat16 [16384, 28672], P('fsdp', 'tp'), may hold values from -0.046875 to 0.046875
- down_weight: bfloat16 [28672, 16384], P('tp', 'fsdp'), may hold values from -0.03125 to 0.03125
Outputs:
- layer_out: bfloat16 [80, 16384], P('tp', 'fsdp')
All inputs are finite; a program needn't handle non-finite values.
Results may differ from a plain program's by a relative error of at most 0.019.
Values may be sent and summed in bfloat16 or wider, within the bound.
No kernel may reach another device: no remote copies, remote signals or barrier semaphores. Data moves between devices by JAX's collectives and lax.ppermute only.
A program may use at most 128 MiB of HBM per device.

v0:
```python
import jax
import jax.numpy as jnp
from jax import lax
from jax.sharding import PartitionSpec as P


def per_device(tokens, gate_weight, up_weight, down_weight):
    segment = lax.all_gather(tokens, "tp", axis=0, tiled=True)
    gate_part = jnp.dot(segment, gate_weight, preferred_element_type=jnp.float32)
    up_part = jnp.dot(segment, up_weight, preferred_element_type=jnp.float32)
    partials = jnp.stack([gate_part, up_part])
    summed = lax.psum_scatter(partials, "fsdp", scatter_dimension=2, tiled=True)
    hidden = (jax.nn.silu(summed[0]) * summed[1]).astype(jnp.bfloat16)
    outputs = jnp.dot(
        lax.all_gather(hidden, "fsdp", axis=1, tiled=True),
        down_weight,
        preferred_element_type=jnp.float32,
    )
    return lax.psum_scatter(outputs.astype(jnp.bfloat16), "tp", scatter_dimension=0, tiled=True)


def solution(mesh):
    placed = (P("tp", "fsdp"), P("fsdp", "tp"), P("fsdp", "tp"), P("tp", "fsdp"))
    return jax.shard_map(
        per_device, mesh=mesh, in_specs=placed, out_specs=P("tp", "fsdp"), check_vma=False
    )
```

profile of v0, /device:TPU:0, one launch (start us, length us, event | category | flops | bytes accessed | tf_op | source)
XLA Modules:
  0.0 188.8 jit_solution(4013773835530704543)
XLA Ops:
  6.5 0.0 reduce-scatter.2.cloned.1.call-start
  6.5 11.3 %all-gather = bf16[4,20,2048]{2,1,0:T(8,128)(2,1)S(1)} all-gather(bf16[1,20,2048]{2,1,0:T(8,128)(2,1)} %bitcast.22), channel_id=1, replica_groups=mesh['fsdp'=8,'tp'=4] {'tp'}, dimensions={0}, use_global_device_ids=true | all-gather | bytes 409600 | tf_op jit(solution)/shard_map/all_gather | solution.py:8
  17.9 0.1 reshape.1
  17.9 12.0 %convolution_bitcast_fusion = f32[1,80,7168]{2,1,0:T(8,128)S(1)} fusion(bf16[80,2048]{1,0:T(8,128)(2,1)S(1)} %reshape.1, bf16[2048,7168]{1,0:T(8,128)(2,1)} %param.6), kind=kOutput, calls=%fused_computation | convolution fusion | flops 2348810240 | bytes 31981568 | tf_op jit(solution)/shard_map/dot_general | solution.py:10
  29.9 12.0 %convolution_bitcast_fusion.1 = f32[1,80,7168]{2,1,0:T(8,128)S(1)} fusion(bf16[80,2048]{1,0:T(8,128)(2,1)S(1)} %reshape.1, bf16[2048,7168]{1,0:T(8,128)(2,1)} %param.5), kind=kOutput, calls=%fused_computation.1 | convolution fusion | flops 2348810240 | bytes 31981568 | tf_op jit(solution)/shard_map/dot_general | solution.py:9
  42.0 2.4 %pad_maximum_fusion = f32[2,80,7168]{2,1,0:T(8,128)} fusion(f32[1,80,7168]{2,1,0:T(8,128)S(1)} %convolution_bitcast_fusion, f32[1,80,7168]{2,1,0:T(8,128)S(1)} %convolution_bitcast_fusion.1), kind=kLoop, calls=%fused_computation.2 | loop fusion | flops 1146880 | bytes 9175040 | tf_op jit(solution)/shard_map/stack | solution.py:11
  44.3 0.0 reduce-scatter.2.cloned.1.call-update
  44.4 0.0 all-gather.3.cloned.1.call-start
  44.4 54.0 %reduce-scatter.2.cloned.1.call-done = f32[2,80,896]{2,1,0:T(8,128)} async-done(((f32[2,80,7168]{2,1,0:T(8,128)}), f32[2,80,896]{2,1,0:T(8,128)}) %reduce-scatter.2.cloned.1.call-update) | async-done | bytes 573456 | tf_op jit(solution)/shard_map/reduce_scatter | solution.py:12
  98.4 1.8 fusion.1
  100.2 0.0 all-gather.3.cloned.1.call-update
  100.2 0.0 copy-start
  100.2 0.0 all-reduce.3.cloned.1.call-start
  100.3 21.4 %all-gather.3.cloned.1.call-done = bf16[80,7168]{1,0:T(8,128)(2,1)} async-done(((bf16[80,896]{1,0:T(8,128)(2,1)}), bf16[80,7168]{1,0:T(8,128)(2,1)}) %all-gather.3.cloned.1.call-update) | async-done | bytes 1146896 | tf_op jit(solution)/shard_map/all_gather | solution.py:15
  121.7 15.6 %convolution_convert_fusion = bf16[80,2048]{1,0:T(8,128)(2,1)} fusion(bf16[80,7168]{1,0:T(8,128)(2,1)} %all-gather.3.cloned.1.call-done, bf16[7168,2048]{1,0:T(8,128)(2,1)} %param.7), kind=kOutput, calls=%fused_computation.3 | convolution fusion | flops 2348974080 | bytes 30834688 | tf_op jit(solution)/shard_map/dot_general | solution.py:14
  137.3 0.0 all-reduce.3.cloned.1.call-update
  137.3 0.0 copy-done
  137.3 0.6 dynamic-slice
  138.6 42.1 %all-reduce.3.cloned.1.call-done = bf16[80,2048]{1,0:T(8,128)(2,1)} async-done(((bf16[80,2048]{1,0:T(8,128)(2,1)}), bf16[80,2048]{1,0:T(8,128)(2,1)}) %all-reduce.3.cloned.1.call-update) | async-done | bytes 327696
  180.7 1.6 constant_dynamic-slice_fusion
Async XLA Ops:
  6.5 91.9 %reduce-scatter.2.cloned.1.call-start = ((), (), s32[]{:S(2)}) async-start(), calls=%async_computation.1 | async-start | bytes 5160960 | tf_op jit(solution)/shard_map/reduce_scatter | solution.py:12
  44.4 77.3 %all-gather.3.cloned.1.call-start = ((), (), s32[]{:S(2)}) async-start(), calls=%async_computation.2 | async-start | bytes 1290240 | tf_op jit(solution)/shard_map/all_gather | solution.py:15
  100.2 37.1 %copy-start = (u32[32]{0:T(128)S(1)}, u32[32]{0:T(128)}, u32[]{:S(2)}) copy-start(u32[32]{0:T(128)} %constant.5) | copy-start | bytes 388
  100.2 80.4 %all-reduce.3.cloned.1.call-start = ((), (), s32[]{:S(2)}) async-start(), calls=%async_computation.3 | async-start | bytes 655360
Sparse Core Ops, SparseCore 0:
  44.5 53.8 reduce-scatter.1
  100.3 21.2 all-gather.2
  137.4 43.1 all-reduce.2
where the time goes:
time: 189 us
  waiting for transfers between devices  118 us (62%)
  matrix products  39.6 us (21%)
  between operations  13.8 us (7%)
  blocking collectives  11.3 us (6%)
  other arithmetic  4.16 us (2%)
  local copies, waits for them, and re-layouts  2.23 us (1%)
    reduce_scatter x1, waiting for transfers between devices, per_device(): summed = lax.psum_scatter(partials, 'fsdp', scatter_dimension=2, tiled=True)  54 us
    unnamed x4, waiting for transfers between devices  42.2 us
    all_gather x1, waiting for transfers between devices, per_device(): lax.all_gather(hidden, 'fsdp', axis=1, tiled=True)  21.4 us
    dot_general x1, matrix products, per_device(): jnp.dot(lax.all_gather(hidden, 'fsdp', axis=1, tiled=True), down_weight,...  15.6 us
    dot_general x1, matrix products, per_device(): up_part = jnp.dot(segment, up_weight, preferred_element_type=jnp.float32)  12 us
    dot_general x1, matrix products, per_device(): jnp.dot(segment, gate_weight, preferred_element_type=jnp.float32)  12 us
    all_gather x1, blocking collectives, per_device(): segment = lax.all_gather(tokens, 'tp', axis=0, tiled=True)  11.3 us
  transfers between devices with their start and end apart: 3, of which 3 were waited for; matrix products, arithmetic and copies ran while one was open for 0% of the time, Pallas kernels for 0%

commit v1 on v0

--- a/solution.py
+++ b/solution.py
@@ -5,7 +5,12 @@
 
 
 def per_device(tokens, gate_weight, up_weight, down_weight):
-    segment = lax.all_gather(tokens, "tp", axis=0, tiled=True)
+    ring = [tokens]
+    for hop in range(3):
+        ring.append(lax.ppermute(ring[-1], "tp", [(dev, (dev + 1) % 4) for dev in range(4)]))
+    segment = jnp.roll(
+        jnp.concatenate(ring[::-1], axis=0), (lax.axis_index("tp") + 1) * ring[0].shape[0], axis=0
+    )
     gate_part = jnp.dot(segment, gate_weight, preferred_element_type=jnp.float32)
     up_part = jnp.dot(segment, up_weight, preferred_element_type=jnp.float32)
     partials = jnp.stack([gate_part, up_part])

time: 189 us -> 198 us (1.048)
  waiting for transfers between devices: 118 us -> 132 us
  blocking collectives: 11.3 us -> 0 us
  starting transfers between devices: 0.09 us -> 3.92 us
  local copies, waits for them, and re-layouts: 2.23 us -> 4.57 us
    ppermute x0 -> x3, waiting for transfers between devices: none -> 14.1 us  [per_device(): lax.ppermute(ring[-1], 'tp', [(dev, (dev + 1) % 4) for dev in range(4)])]
    all_gather x1 -> x0, blocking collectives: 11.3 us -> none  [per_device(): segment = lax.all_gather(tokens, 'tp', axis=0, tiled=True)]
    ppermute x0 -> x3, starting transfers between devices: none -> 3.84 us  [per_device(): lax.ppermute(ring[-1], 'tp', [(dev, (dev + 1) % 4) for dev in range(4)])]
    concatenate x0 -> x1, local copies, waits for them, and re-layouts: none -> 2.41 us  [per_device(): jnp.roll(jnp.concatenate(ring[::-1], axis=0), (lax.axis_index('tp') + 1)...]
  transfers between devices with their start and end apart: 3 -> 6, of which waited for: 3 -> 6; matrix products, arithmetic and copies ran while one was open for 0% -> 0% of each run, Pallas kernels for 0% -> 0%
where the time goes in v1:
time: 198 us
  waiting for transfers between devices  132 us (67%)
  matrix products  39.6 us (20%)
  between operations  13.8 us (7%)
  local copies, waits for them, and re-layouts  4.57 us (2%)
  other arithmetic  4.28 us (2%)
  starting transfers between devices  3.92 us (2%)
    reduce_scatter x1, waiting for transfers between devices, per_device(): summed = lax.psum_scatter(partials, 'fsdp', scatter_dimension=2, tiled=True)  54.3 us
    unnamed x4, waiting for transfers between devices  42.2 us
    all_gather x1, waiting for transfers between devices, per_device(): lax.all_gather(hidden, 'fsdp', axis=1, tiled=True)  21.4 us
    dot_general x1, matrix products, per_device(): jnp.dot(lax.all_gather(hidden, 'fsdp', axis=1, tiled=True), down_weight,...  15.6 us
    ppermute x3, waiting for transfers between devices, per_device(): lax.ppermute(ring[-1], 'tp', [(dev, (dev + 1) % 4) for dev in range(4)])  14.1 us
    dot_general x1, matrix products, per_device(): up_part = jnp.dot(segment, up_weight, preferred_element_type=jnp.float32)  12 us
    dot_general x1, matrix products, per_device(): jnp.dot(segment, gate_weight, preferred_element_type=jnp.float32)  12 us
  transfers between devices with their start and end apart: 6, of which 6 were waited for; matrix products, arithmetic and copies ran while one was open for 0% of the time, Pallas kernels for 0%

profile of v1, /device:TPU:0, one launch (start us, length us, event | category | flops | bytes accessed | tf_op | source)
XLA Modules:
  0.0 198.2 jit_solution(11291952436049780912)
XLA Ops:
  6.5 0.0 reduce-scatter.2.cloned.1.call-start
  6.5 3.0 %collective-permute-start = (bf16[20,2048]{1,0:T(8,128)(2,1)}, bf16[20,2048]{1,0:T(8,128)(2,1)S(1)}, u32[]{:S(2)}, u32[]{:S(2)}) collective-permute-start(bf16[20,2048]{1,0:T(8,128)(2,1)} %param.4), channel_id=1, source_target_pairs={{0,1},{1,2},{2,3},{3,0},{4,5},{5,6},{6,7},{7,4},{8,9},{9,10},{10,1... | collective-permute-start | bytes 245768 | tf_op jit(solution)/shard_map/ppermute | solution.py:10
  9.5 4.0 %collective-permute-done = bf16[20,2048]{1,0:T(8,128)(2,1)S(1)} collective-permute-done((bf16[20,2048]{1,0:T(8,128)(2,1)}, bf16[20,2048]{1,0:T(8,128)(2,1)S(1)}, u32[]{:S(2)}, u32[]{:S(2)}) %collective-permute-start) | collective-permute-done | bytes 81952 | tf_op jit(solution)/shard_map/ppermute | solution.py:10
  13.5 0.9 collective-permute-start.1
  14.3 4.6 %collective-permute-done.1 = bf16[20,2048]{1,0:T(8,128)(2,1)S(1)} collective-permute-done((bf16[20,2048]{1,0:T(8,128)(2,1)S(1)}, bf16[20,2048]{1,0:T(8,128)(2,1)S(1)}, u32[]{:S(2)}, u32[]{:S(2)}) %collective-permute-start.1) | collective-permute-done | bytes 81952 | tf_op jit(solution)/shard_map/ppermute | solution.py:10
  19.0 0.0 collective-permute-start.2
  19.0 5.5 %collective-permute-done.2 = bf16[20,2048]{1,0:T(8,128)(2,1)S(1)} collective-permute-done((bf16[20,2048]{1,0:T(8,128)(2,1)S(1)}, bf16[20,2048]{1,0:T(8,128)(2,1)S(1)}, u32[]{:S(2)}, u32[]{:S(2)}) %collective-permute-start.2) | collective-permute-done | bytes 81952 | tf_op jit(solution)/shard_map/ppermute | solution.py:10
  24.5 2.4 %concatenate.6 = bf16[160,2048]{1,0:T(8,128)(2,1)S(1)} concatenate(bf16[20,2048]{1,0:T(8,128)(2,1)S(1)} %collective-permute-done.2, bf16[20,2048]{1,0:T(8,128)(2,1)S(1)} %collective-permute-done.1, bf16[20,2048]{1,0:T(8,128)(2,1)S(1)} %collective-permute-done, bf16[20,2048]{1,0:T(8,128)(2,1)} %param.4, bf16[20,2048]{1,0:T(8,128)(2,1)S(1)} %collective-permute-done.2, ...), dimensions={0} | concatenate | bytes 1310720 | tf_op jit(solution)/shard_map/jit(_roll_dynamic)/concatenate | solution.py:11
  26.9 12.0 %convolution_bitcast_fusion.1 = f32[1,80,7168]{2,1,0:T(8,128)S(1)} fusion(bf16[2048,7168]{1,0:T(8,128)(2,1)} %param.5, bf16[160,2048]{1,0:T(8,128)(2,1)S(1)} %concatenate.6, s32[]{:T(128)S(6)} %select_n.14), kind=kOutput, calls=%fused_computation.1 | convolution fusion | flops 2348810240 | bytes 31981572 | tf_op jit(solution)/shard_map/dot_general | solution.py:14
  38.9 12.0 %convolution_bitcast_fusion = f32[1,80,7168]{2,1,0:T(8,128)S(1)} fusion(bf16[2048,7168]{1,0:T(8,128)(2,1)} %param.6, bf16[160,2048]{1,0:T(8,128)(2,1)S(1)} %concatenate.6, s32[]{:T(128)S(6)} %select_n.14), kind=kOutput, calls=%fused_computation | convolution fusion | flops 2348810240 | bytes 31981572 | tf_op jit(solution)/shard_map/dot_general | solution.py:15
  50.9 2.5 %pad_maximum_fusion = f32[2,80,7168]{2,1,0:T(8,128)} fusion(f32[1,80,7168]{2,1,0:T(8,128)S(1)} %convolution_bitcast_fusion, f32[1,80,7168]{2,1,0:T(8,128)S(1)} %convolution_bitcast_fusion.1), kind=kLoop, calls=%fused_computation.2 | loop fusion | flops 1146880 | bytes 9175040 | tf_op jit(solution)/shard_map/stack | solution.py:16
  53.4 0.0 reduce-scatter.2.cloned.1.call-update
  53.4 0.0 all-gather.2.cloned.1.call-start
  53.5 54.3 %reduce-scatter.2.cloned.1.call-done = f32[2,80,896]{2,1,0:T(8,128)} async-done(((f32[2,80,7168]{2,1,0:T(8,128)}), f32[2,80,896]{2,1,0:T(8,128)}) %reduce-scatter.2.cloned.1.call-update) | async-done | bytes 573456 | tf_op jit(solution)/shard_map/reduce_scatter | solution.py:17
  107.8 1.8 fusion.3
  109.6 0.0 all-gather.2.cloned.1.call-update
  109.7 0.0 copy-start
  109.7 0.0 all-reduce.3.cloned.1.call-start
  109.7 21.4 %all-gather.2.cloned.1.call-done = bf16[80,7168]{1,0:T(8,128)(2,1)} async-done(((bf16[80,896]{1,0:T(8,128)(2,1)}), bf16[80,7168]{1,0:T(8,128)(2,1)}) %all-gather.2.cloned.1.call-update) | async-done | bytes 1146896 | tf_op jit(solution)/shard_map/all_gather | solution.py:20
  131.1 15.6 %convolution_convert_fusion = bf16[80,2048]{1,0:T(8,128)(2,1)} fusion(bf16[80,7168]{1,0:T(8,128)(2,1)} %all-gather.2.cloned.1.call-done, bf16[7168,2048]{1,0:T(8,128)(2,1)} %param.7), kind=kOutput, calls=%fused_computation.3 | convolution fusion | flops 2348974080 | bytes 30834688 | tf_op jit(solution)/shard_map/dot_general | solution.py:19
  146.7 0.0 all-reduce.3.cloned.1.call-update
  146.7 0.0 copy-done
  146.8 0.6 dynamic-slice
  148.0 42.1 %all-reduce.3.cloned.1.call-done = bf16[80,2048]{1,0:T(8,128)(2,1)} async-done(((bf16[80,2048]{1,0:T(8,128)(2,1)}), bf16[80,2048]{1,0:T(8,128)(2,1)}) %all-reduce.3.cloned.1.call-update) | async-done | bytes 327696
  190.1 1.6 constant_dynamic-slice_fusion
Async XLA Ops:
  6.5 101.3 %reduce-scatter.2.cloned.1.call-start = ((), (), s32[]{:S(2)}) async-start(), calls=%async_computation.1 | async-start | bytes 5160960 | tf_op jit(solution)/shard_map/reduce_scatter | solution.py:17
  6.5 6.9 %collective-permute-start = (bf16[20,2048]{1,0:T(8,128)(2,1)}, bf16[20,2048]{1,0:T(8,128)(2,1)S(1)}, u32[]{:S(2)}, u32[]{:S(2)}) collective-permute-start(bf16[20,2048]{1,0:T(8,128)(2,1)} %param.4), channel_id=1, source_target_pairs={{0,1},{1,2},{2,3},{3,0},{4,5},{5,6},{6,7},{7,4},{8,9},{9,10},{10,1... | collective-permute-start | bytes 245768 | tf_op jit(solution)/shard_map/ppermute | solution.py:10
  13.5 5.5 %collective-permute-start.1 = (bf16[20,2048]{1,0:T(8,128)(2,1)S(1)}, bf16[20,2048]{1,0:T(8,128)(2,1)S(1)}, u32[]{:S(2)}, u32[]{:S(2)}) collective-permute-start(bf16[20,2048]{1,0:T(8,128)(2,1)S(1)} %collective-permute-done), channel_id=1, source_target_pairs={{0,1},{1,2},{2,3},{3,0},{4,5},{5,6},{6,7},{7,4},{8,9},{9,10},{10,1... | collective-permute-start | bytes 245768 | tf_op jit(solution)/shard_map/ppermute | solution.py:10
  19.0 5.5 %collective-permute-start.2 = (bf16[20,2048]{1,0:T(8,128)(2,1)S(1)}, bf16[20,2048]{1,0:T(8,128)(2,1)S(1)}, u32[]{:S(2)}, u32[]{:S(2)}) collective-permute-start(bf16[20,2048]{1,0:T(8,128)(2,1)S(1)} %collective-permute-done.1), channel_id=1, source_target_pairs={{0,1},{1,2},{2,3},{3,0},{4,5},{5,6},{6,7},{7,4},{8,9},{9,10},{10,1... | collective-permute-start | bytes 245768 | tf_op jit(solution)/shard_map/ppermute | solution.py:10
  53.4 77.7 %all-gather.2.cloned.1.call-start = ((), (), s32[]{:S(2)}) async-start(), calls=%async_computation.2 | async-start | bytes 1290240 | tf_op jit(solution)/shard_map/all_gather | solution.py:20
  109.7 37.1 %copy-start = (u32[32]{0:T(128)S(1)}, u32[32]{0:T(128)}, u32[]{:S(2)}) copy-start(u32[32]{0:T(128)} %constant.32) | copy-start | bytes 388
  109.7 80.4 %all-reduce.3.cloned.1.call-start = ((), (), s32[]{:S(2)}) async-start(), calls=%async_computation.3 | async-start | bytes 655360
Sparse Core Ops, SparseCore 0:
  53.6 54.2 reduce-scatter.1
  109.8 21.2 all-gather.1
  146.9 43.1 all-reduce.2
